TPU v7x, 32 devices: a whole 2x2x4 slice. The times are simulated.
32 devices in a mesh: date: 16 (over z, y, x), prod: 2 (over core).
Axes of the slice: x: 2, y: 2, z: 4, core: 2. Of those that a mesh axis runs over, the one named last changes fastest.
Arguments:
- daily_sales: float32 [256, 512, 128], P('prod', 'date'), may hold values from -2.5 to 2.5
- week_id: int32 [512], P('date'), may hold values from 0 to 102, never falling along the last dimension, each value on 1 to 7 neighbouring positions
- month_id: int32 [512], P('date'), may hold values from 0 to 21, never falling along the last dimension, each value on 1 to 31 neighbouring positions
- year_id: int32 [512], P('date'), may hold values from 0 to 1, never falling along the last dimension, each value on 1 to 366 neighbouring positions
Outputs:
- running: float32 [256, 512, 128], P('prod', 'date')
- week_total: float32 [256, 512, 128], P('prod', 'date')
- month_total: float32 [256, 512, 128], P('prod', 'date')
- year_total: float32 [256, 512, 128], P('prod', 'date')
- store_rollup: float32 [4, 512, 128], P(None, 'date')
Inputs may be any that keep to these rules, and one draw needn't show every extreme that they name: `week_id`: starts at 0 and never falls along the dates; each week covers 1 to 7 consecutive dates and some cover exactly 7. `month_id`: starts at 0 and never falls along the dates; each month covers 1 to 31 consecutive dates and some cover exactly 31; months need not line up with weeks. `year_id`: starts at 0 and never falls along the dates; each year covers 1 to 366 consecutive dates and some cover exactly 366; years need not line up with weeks or months.
All inputs are finite; a program needn't handle non-finite values.
Results may differ from a plain program's by a relative error of at most 0.000094.
Values sent between devices are 32-bit elements.
A program may use at most 64 MiB of HBM per device.

v0:
```python
import functools

import jax
import jax.numpy as jnp
from jax import lax
from jax.experimental import pallas as pl
from jax.experimental.pallas import tpu as pltpu
from jax.sharding import PartitionSpec as P

MESH = pl.DeviceIdType.MESH
F32 = jnp.float32


def id_column(ids, span, lanes):
    where = lax.broadcasted_iota(jnp.int32, (span, lanes), 0)
    column = jnp.zeros((span, lanes), jnp.int32)
    for t in range(span):
        column = jnp.where(where == t, ids[t], column)
    return column


def id_row(ids, span, lanes):
    where = lax.broadcasted_iota(jnp.int32, (span, lanes), 1) % span
    row = jnp.zeros((span, lanes), jnp.int32)
    for t in range(span):
        row = jnp.where(where == t, ids[t], row)
    return row


def edge_masks(ids, span, lanes):
    column = id_column(ids, span, lanes)
    return (column == ids[0]).astype(F32), (column == ids[span - 1]).astype(F32)


def stack_rows(values, rows, lanes):
    where = lax.broadcasted_iota(jnp.int32, (rows, lanes), 0)
    tile = jnp.zeros((rows, lanes), F32)
    for i, value in enumerate(values):
        tile = jnp.where(where == i, value, tile)
    return tile


def exchange_kernel(
    n, n_prod, slices, loads, wide,
    week_hbm, month_hbm, year_hbm, x_hbm,
    carry, near, meta_hbm, mixer_hbm, gains_hbm,
    week, month, year, meta, mixer, gains,
    x, send1, recv1, send2, edges, seen, summed, parts,
    ids_sem, out_sem, sum_s, sum_r, load_sem, id_s, id_r, s1_sem, r1_sem, s2_sem, r2_sem, sib_s, sib_r, near_s, near_r,
):
    me = lax.axis_index("date")
    core = lax.axis_index("prod")
    columns, span, lanes = x.shape
    rows = columns // slices
    chunk = columns // loads
    last = span - 1
    loaded = [
        pltpu.make_async_copy(
            x_hbm.at[pl.ds(i * chunk, chunk)], x.at[pl.ds(i * chunk, chunk)], load_sem.at[i]
        )
        for i in range(loads)
    ]
    for copy in loaded:
        copy.start()
    fetched = [
        pltpu.make_async_copy(source, target, ids_sem.at[i])
        for i, (source, target) in enumerate(
            ((year_hbm, year), (week_hbm, week), (month_hbm, month))
        )
    ]
    for copy in fetched:
        copy.start()
    barrier = pltpu.get_barrier_semaphore()
    for d in range(1, n):
        pl.semaphore_signal(
            barrier, inc=1, device_id=(lax.rem(me + d, n), core), device_id_type=MESH
        )
    for d in range(1, n_prod):
        pl.semaphore_signal(
            barrier, inc=1, device_id=(me, lax.rem(core + d, n_prod)), device_id_type=MESH
        )
    for copy in fetched:
        copy.wait()
    lane = lax.broadcasted_iota(jnp.int32, (1, lanes), 1)
    ids = jnp.zeros((1, lanes), F32)
    for i, v in enumerate((year[0], year[last], week[0], week[last], month[0], month[last])):
        ids = jnp.where(lane == i, v.astype(F32), ids)
    seen[me] = ids
    head_y, tail_y = edge_masks(year, span, lanes)

    def outer_sums(s, total):
        block = x[pl.ds(pl.multiple_of(s * rows, rows), rows)]
        send1[s, 0] = jnp.sum(block * head_y[None], axis=1)
        send1[s, 1] = jnp.sum(block * tail_y[None], axis=1)
        if wide:
            send1[s, 2] = jnp.sum(block, axis=1)
        return total + jnp.sum(block, axis=0)

    total = jnp.zeros((span, lanes), F32)
    per_load = slices // loads
    for i in range(loads):
        loaded[i].wait()
        total = lax.fori_loop(i * per_load, (i + 1) * per_load, outer_sums, total)
    recv1[me] = send1[lax.rem(me, slices)]
    pl.semaphore_wait(barrier, n - 1 + n_prod - 1)

    def to_all(source, target, send_sem, recv_sem):
        copies = []
        for d in sorted(range(1, n), key=lambda d: -min(d, n - d)):
            peer = lax.rem(me + d, n)
            copy = pltpu.make_async_remote_copy(
                src_ref=source(peer), dst_ref=target.at[me],
                send_sem=send_sem.at[peer], recv_sem=recv_sem.at[me],
                device_id=(peer, core), device_id_type=MESH,
            )
            copy.start()
            copies.append(copy)
        return copies

    def arrived(target, send_sem, recv_sem):
        for d in range(1, n):
            peer = lax.rem(me + d, n)
            pltpu.make_async_remote_copy(
                src_ref=target.at[me], dst_ref=target.at[peer],
                send_sem=send_sem.at[peer], recv_sem=recv_sem.at[peer],
                device_id=(peer, core), device_id_type=MESH,
            ).wait_recv()

    sent = to_all(lambda peer: seen.at[me], seen, id_s, id_r)
    sent += to_all(lambda peer: send1.at[lax.rem(peer, slices)], recv1, s1_sem, r1_sem)

    head_w, tail_w = edge_masks(week, span, lanes)
    head_m, tail_m = edge_masks(month, span, lanes)
    summed[me] = stack_rows(
        [jnp.sum(total, axis=0, keepdims=True)]
        + [
            jnp.sum(total * m, axis=0, keepdims=True)
            for m in (head_y, tail_y, head_w, tail_w, head_m, tail_m)
        ],
        8, lanes,
    )
    left, right = lax.rem(me + n - 1, n), lax.rem(me + 1, n)

    def edge_sums(level, head, tail):
        def inner_sums(s, nothing):
            at = pl.ds(pl.multiple_of(s * rows, rows), rows)
            block = x[at]
            edges[0, level, at] = jnp.sum(block * tail[None], axis=1)
            edges[1, level, at] = jnp.sum(block * head[None], axis=1)
            return nothing

        lax.fori_loop(0, slices, inner_sums, 0)

    linked = (me < n - 1, me > 0)

    def edge_copy(side, level):
        return pltpu.make_async_remote_copy(
            src_ref=edges.at[side, level], dst_ref=near.at[side, level],
            send_sem=near_s.at[side, level], recv_sem=near_r.at[side, level],
            device_id=((right, left)[side], core), device_id_type=MESH,
        )

    def edge_send(side, level):
        @pl.when(linked[side])
        def _():
            edge_copy(side, level).start()

        @pl.when(jnp.logical_not(linked[side]))
        def _():
            pltpu.make_async_copy(
                edges.at[side, level], near.at[1 - side, level], near_r.at[1 - side, level]
            ).start()

    edge_sums(0, head_w, tail_w)
    sent += to_all(lambda peer: summed.at[me], summed, sum_s, sum_r)
    edge_send(0, 0)
    edge_send(1, 0)
    edge_sums(1, head_m, tail_m)
    edge_send(0, 1)

    sub = lax.broadcasted_iota(jnp.int32, (span, 3 * span), 0)
    place = lax.broadcasted_iota(jnp.int32, (span, 3 * span), 1) % span
    mixer[0:span] = jnp.where(place <= sub, 1.0, 0.0).astype(mixer.dtype)
    for k, level in enumerate((week, month, year)):
        same = id_column(level, span, 3 * span) == id_row(level, span, 3 * span)
        mixer[(k + 1) * span : (k + 2) * span] = jnp.where(same, 1.0, 0.0).astype(mixer.dtype)

    arrived(seen, id_s, id_r)
    low = [jnp.broadcast_to(seen[b][:, 0:1], (rows, lanes)) for b in range(n)]
    top = [jnp.broadcast_to(seen[b][:, 1:2], (rows, lanes)) for b in range(n)]
    arrived(recv1, s1_sem, r1_sem)
    zero = jnp.zeros((rows, lanes), F32)
    running, into = zero, zero
    brought = []
    for b in range(n):
        send2[b, 0] = running
        brought.append(into)
        if wide:
            send2[b, 1] = into
        if b + 1 < n:
            head, tail = recv1[b, 0], recv1[b, 1]
            one = low[b] == top[b]
            running = running + (recv1[b, 2] if wide else head + jnp.where(one, 0.0, tail))
            into = jnp.where(top[b] == low[b + 1], tail + jnp.where(one, into, 0.0), 0.0)
    back = zero
    for b in reversed(range(n)):
        one = low[b] == top[b]
        if wide:
            send2[b, 2] = back
        else:
            send2[b, 1] = back + jnp.where(one, brought[b], 0.0)
        if b > 0:
            held = recv1[b, 0] + jnp.where(one, back, 0.0)
            back = jnp.where(top[b - 1] == low[b], held, 0.0)
    sent += to_all(lambda peer: send2.at[peer], carry, s2_sem, r2_sem)
    edge_send(1, 1)
    kept = pltpu.make_async_copy(send2.at[me], carry.at[me], out_sem.at[0])
    kept.start()

    def gain(there, lane_seen, own, where):
        value = jnp.broadcast_to(seen[there][:, lane_seen : lane_seen + 1], (1, lanes))
        return jnp.where(jnp.logical_and(value == own.astype(F32), where), 1.0, 0.0)

    gains[0] = head_w * gain(left, 3, week[0], me > 0)
    gains[1] = tail_w * gain(right, 2, week[last], me < n - 1)
    gains[2] = head_m * gain(left, 5, month[0], me > 0)
    gains[3] = tail_m * gain(right, 4, month[last], me < n - 1)
    gains[4] = head_y if wide else head_y * jnp.where(year[0] == year[last], 0.0, 1.0)
    gains[5] = tail_y
    leaving = [
        pltpu.make_async_copy(mixer, mixer_hbm, out_sem.at[1]),
        pltpu.make_async_copy(gains, gains_hbm, out_sem.at[2]),
    ]
    for copy in leaving:
        copy.start()

    arrived(summed, sum_s, sum_r)
    run_sum = jnp.zeros((1, lanes), F32)
    in_sum, back_sum = run_sum, run_sum
    low_me, top_me = low[0][0:1] * 0.0, top[0][0:1] * 0.0
    low_me = low_me + year[0].astype(F32)
    top_me = top_me + year[last].astype(F32)
    for b in range(n):
        tile = summed[b]
        run_sum = run_sum + jnp.where(b < me, tile[0:1], 0.0)
        inside = jnp.logical_and(top[b][0:1] == low_me, b < me)
        in_sum = in_sum + jnp.where(inside, tile[2:3], 0.0)
        inside = jnp.logical_and(low[b][0:1] == top_me, b > me)
        back_sum = back_sum + jnp.where(inside, tile[1:2], 0.0)
    if wide:
        first_sum, last_sum = in_sum, back_sum
    else:
        first_sum = run_sum
        last_sum = back_sum + jnp.where(low_me == top_me, in_sum, 0.0)
    from_left, from_right = summed[left], summed[right]
    parts[core, 0:8] = stack_rows(
        [
            run_sum, first_sum, last_sum,
            from_left[4:5], from_left[6:7], from_right[3:4], from_right[5:6],
        ],
        8, lanes,
    )
    parts[core, 8 : 8 + span] = total
    shared = []
    for d in range(1, n_prod):
        peer = lax.rem(core + d, n_prod)
        copy = pltpu.make_async_remote_copy(
            src_ref=parts.at[core], dst_ref=parts.at[core],
            send_sem=sib_s.at[peer], recv_sem=sib_r.at[core],
            device_id=(me, peer), device_id_type=MESH,
        )
        copy.start()
        shared.append(copy)
    for d in range(1, n_prod):
        peer = lax.rem(core + d, n_prod)
        pltpu.make_async_remote_copy(
            src_ref=parts.at[core], dst_ref=parts.at[peer],
            send_sem=sib_s.at[peer], recv_sem=sib_r.at[peer],
            device_id=(me, peer), device_id_type=MESH,
        ).wait_recv()
    whole = parts[0]
    for i in range(1, n_prod):
        whole = whole + parts[i]
    meta[...] = whole
    last_out = pltpu.make_async_copy(meta, meta_hbm, out_sem.at[3])
    last_out.start()
    for copy in sent + shared:
        copy.wait_send()
    kept.wait()
    for copy in leaving:
        copy.wait()
    for side in range(2):
        for level in range(2):
            edge_copy(side, level).wait_recv()

            @pl.when(linked[side])
            def _():
                edge_copy(side, level).wait_send()

    arrived(carry, s2_sem, r2_sem)
    last_out.wait()


def exchange(n, n_prod, slices, wide, week, month, year, sales):
    columns, span, lanes = sales.shape
    rows = columns // slices
    loads = 4 if slices % 4 == 0 else 1
    anywhere = pl.BlockSpec(memory_space=pl.ANY)
    packet = (n, 3 if wide else 2, rows, lanes)
    dma = pltpu.SemaphoreType.DMA
    return pl.pallas_call(
        functools.partial(exchange_kernel, n, n_prod, slices, loads, wide),
        out_shape=(
            jax.ShapeDtypeStruct(packet, F32),
            jax.ShapeDtypeStruct((2, 2, columns, lanes), F32),
            jax.ShapeDtypeStruct((8 + span, lanes), F32),
            jax.ShapeDtypeStruct((4 * span, 3 * span), jnp.bfloat16),
            jax.ShapeDtypeStruct((6, span, lanes), F32),
        ),
        in_specs=[anywhere] * 4,
        out_specs=(anywhere,) * 5,
        scratch_shapes=[
            pltpu.SMEM((span,), jnp.int32),
            pltpu.SMEM((span,), jnp.int32),
            pltpu.SMEM((span,), jnp.int32),
            pltpu.VMEM((8 + span, lanes), F32),
            pltpu.VMEM((4 * span, 3 * span), jnp.bfloat16),
            pltpu.VMEM((6, span, lanes), F32),
            pltpu.VMEM(sales.shape, F32),
            pltpu.VMEM((slices,) + packet[1:], F32),
            pltpu.VMEM(packet, F32),
            pltpu.VMEM(packet, F32),
            pltpu.VMEM((2, 2, columns, lanes), F32),
            pltpu.VMEM((n, 1, lanes), F32),
            pltpu.VMEM((n, 8, lanes), F32),
            pltpu.VMEM((n_prod, 8 + span, lanes), F32),
            dma((3,)), dma((4,)), dma((n,)), dma((n,)), dma((loads,)), dma((n,)), dma((n,)), dma((n,)), dma((n,)), dma((n,)), dma((n,)),
            dma((n_prod,)), dma((n_prod,)), dma((2, 2)), dma((2, 2)),
        ],
        compiler_params=pltpu.CompilerParams(collective_id=0, has_side_effects=True),
        name="exchange",
    )(week, month, year, sales)


def split3(value):
    high = value.astype(jnp.bfloat16)
    rest = value - high.astype(F32)
    middle = rest.astype(jnp.bfloat16)
    low = (rest - middle.astype(F32)).astype(jnp.bfloat16)
    return jnp.concatenate([high, middle, low], axis=-2)


def apply_kernel(
    wide, steps, x_hbm, carry_hbm, near_hbm, meta_hbm, mixer_hbm, gains_hbm,
    run_hbm, week_hbm, month_hbm, year_hbm, rollup_hbm,
    x, carry, near, meta, mixer, gains, run_out, week_out, month_out, year_out, rollup,
    x_sem, in_sem, out_sem, rollup_sem,
):
    columns, span, lanes = x.shape
    groups, _, rows, _ = carry.shape
    per_step = groups // steps
    block = columns // steps
    small = [
        pltpu.make_async_copy(source, target, in_sem.at[i])
        for i, (source, target) in enumerate(
            (
                (mixer_hbm, mixer), (gains_hbm, gains),
                (carry_hbm.at[pl.ds(0, groups)], carry), (near_hbm, near), (meta_hbm, meta),
            )
        )
    ]
    pieces = [pl.ds(i * block, block) for i in range(steps)]
    loads = [
        pltpu.make_async_copy(x_hbm.at[at], x.at[at], x_sem.at[i]) for i, at in enumerate(pieces)
    ]
    loads[0].start()
    for copy in small:
        copy.start()
    for copy in loads[1:]:
        copy.start()
    for copy in small:
        copy.wait()

    def group(g, nothing):
        base = pl.multiple_of(g * rows, rows)
        at = pl.ds(base, rows)
        left_w, left_m = near[0, 0, at], near[0, 1, at]
        right_w, right_m = near[1, 0, at], near[1, 1, at]
        start = carry[g, 0]
        year_l, year_r = carry[g, 1 if wide else 0], carry[g, 2 if wide else 1]
        for r in range(0, rows, 2):
            parts = split3(x[pl.ds(base + r, 2)])
            both = jnp.concatenate([parts[0], parts[1]], axis=1)
            mixed = jnp.dot(mixer[...], both, preferred_element_type=F32)
            for j in range(2):
                q = r + j
                row = slice(q, q + 1)
                own = mixed[:, j * lanes : (j + 1) * lanes]
                run_out[base + q] = own[0:span] + start[row]
                week_out[base + q] = (
                    own[span : 2 * span] + left_w[row] * gains[0] + right_w[row] * gains[1]
                )
                month_out[base + q] = (
                    own[2 * span : 3 * span] + left_m[row] * gains[2] + right_m[row] * gains[3]
                )
                year_out[base + q] = (
                    own[3 * span : 4 * span] + year_l[row] * gains[4] + year_r[row] * gains[5]
                )
        return nothing

    stores = []
    for i, at in enumerate(pieces):
        loads[i].wait()
        lax.fori_loop(i * per_step, (i + 1) * per_step, group, 0, unroll=per_step <= 2)
        for k, (source, target) in enumerate(
            (
                (run_out, run_hbm), (week_out, week_hbm),
                (month_out, month_hbm), (year_out, year_hbm),
            )
        ):
            copy = pltpu.make_async_copy(source.at[at], target.at[at], out_sem.at[i, k])
            copy.start()
            stores.append(copy)
        if i == 0:
            mixed = jnp.dot(mixer[...], split3(meta[8 : 8 + span]), preferred_element_type=F32)
            rollup[0] = mixed[0:span] + meta[0:1]
            rollup[1] = mixed[span : 2 * span] + meta[3:4] * gains[0] + meta[5:6] * gains[1]
            rollup[2] = mixed[2 * span : 3 * span] + meta[4:5] * gains[2] + meta[6:7] * gains[3]
            rollup[3] = mixed[3 * span : 4 * span] + meta[1:2] * gains[4] + meta[2:3] * gains[5]
            copy = pltpu.make_async_copy(rollup, rollup_hbm, rollup_sem.at[0])
            copy.start()
            stores.append(copy)
    for copy in stores:
        copy.wait()


def apply(slices, wide, sales, carry, near, meta, mixer, gains):
    span, lanes = sales.shape[1:]
    steps = 8 if slices % 8 == 0 else 1
    anywhere = pl.BlockSpec(memory_space=pl.ANY)
    cube_shape = jax.ShapeDtypeStruct(sales.shape, F32)
    cube = pltpu.VMEM(sales.shape, F32)
    dma = pltpu.SemaphoreType.DMA
    return pl.pallas_call(
        functools.partial(apply_kernel, wide, steps),
        out_shape=(cube_shape,) * 4 + (jax.ShapeDtypeStruct((4, span, lanes), F32),),
        in_specs=[anywhere] * 6,
        out_specs=(anywhere,) * 5,
        scratch_shapes=[
            cube,
            pltpu.VMEM((slices,) + carry.shape[1:], F32),
            pltpu.VMEM(near.shape, F32),
            pltpu.VMEM(meta.shape, F32),
            pltpu.VMEM(mixer.shape, mixer.dtype),
            pltpu.VMEM(gains.shape, F32),
            cube, cube, cube, cube,
            pltpu.VMEM((4, span, lanes), F32),
            dma((steps,)), dma((5,)), dma((steps, 4)), dma((1,)),
        ],
        name="apply",
    )(sales, carry, near, meta, mixer, gains)


def solution(mesh):
    n, n_prod = mesh.shape["date"], mesh.shape["prod"]

    def local(sales, week, month, year):
        slices = min(n, sales.shape[0] // 8)
        wide = n * sales.shape[1] // 300 + 1 > 2
        passed = exchange(n, n_prod, slices, wide, week, month, year, sales)
        return apply(slices, wide, sales, *passed)

    return jax.shard_map(
        local,
        mesh=mesh,
        in_specs=(P("prod", "date", None), P("date"), P("date"), P("date")),
        out_specs=(P("prod", "date", None),) * 4 + (P(None, "date", None),),
        check_vma=False,
    )
```

profile of v0, /device:TPU:0, one launch (start us, length us, event | category | flops | bytes accessed | tf_op | source)
XLA Modules:
  0.0 26.0 jit_solution(2632231163322844350)
XLA Ops:
  0.6 19.9 %exchange.1 = (f32[16,2,8,128]{3,2,1,0:T(8,128)}, f32[2,2,128,128]{3,2,1,0:T(8,128)}, f32[40,128]{1,0:T(8,128)}, bf16[128,96]{1,0:T(8,128)(2,1)}, f32[6,32,128]{2,1,0:T(8,128)}) custom-call(s32[32]{0:T(128)} %week_hbm.1, s32[32]{0:T(128)} %month_hbm.1, s32[32]{0:T(128)} %year_hbm.1, f32[128,32,128]{2,1,0:T(8,128)} %x_hbm.3), custom_call_target="tpu_custom_call" | custom-call | tf_op jit(solution)/shard_map/exchange/pallas_call | solution.py:311
  20.5 5.5 %apply.1 = (f32[128,32,128]{2,1,0:T(8,128)}, f32[128,32,128]{2,1,0:T(8,128)}, f32[128,32,128]{2,1,0:T(8,128)}, f32[128,32,128]{2,1,0:T(8,128)}, f32[4,32,128]{2,1,0:T(8,128)}) custom-call(f32[128,32,128]{2,1,0:T(8,128)} %x_hbm.3, f32[16,2,8,128]{3,2,1,0:T(8,128)} %get-tuple-element.10.carry_hbm, f32[2,2,128,128]{3,2,1,0:T(8,128)} %get-tuple-element.11.near_hbm, ...), custom_call_target="tpu_custom_call" | custom-call | tf_op jit(solution)/shard_map/apply/pallas_call | solution.py:444
where the time goes:
time: 26.2 us; the launch traced here: 26 us
  Pallas kernels  25.4 us (97%)
  between operations  0.64 us (2%)
    pallas_call x1, Pallas kernels, exchange(): pl.pallas_call(functools.partial(exchange_kernel, n, n_prod, slices, load...  19.9 us
    pallas_call x1, Pallas kernels, apply(): pl.pallas_call(functools.partial(apply_kernel, wide, steps), out_shape=(c...  5.46 us

commit v1 on v0

v1 whole, which is shorter than its diff:
```python
import functools

import jax
import jax.numpy as jnp
from jax import lax
from jax.experimental import pallas as pl
from jax.experimental.pallas import tpu as pltpu
from jax.sharding import PartitionSpec as P

MESH = pl.DeviceIdType.MESH
F32 = jnp.float32


def id_column(ids, span, lanes):
    where = lax.broadcasted_iota(jnp.int32, (span, lanes), 0)
    column = jnp.zeros((span, lanes), jnp.int32)
    for t in range(span):
        column = jnp.where(where == t, ids[t], column)
    return column


def id_row(ids, span, lanes):
    where = lax.broadcasted_iota(jnp.int32, (span, lanes), 1) % span
    row = jnp.zeros((span, lanes), jnp.int32)
    for t in range(span):
        row = jnp.where(where == t, ids[t], row)
    return row


def edge_masks(ids, span, lanes):
    column = id_column(ids, span, lanes)
    return (column == ids[0]).astype(F32), (column == ids[span - 1]).astype(F32)


def stack_rows(values, rows, lanes):
    where = lax.broadcasted_iota(jnp.int32, (rows, lanes), 0)
    tile = jnp.zeros((rows, lanes), F32)
    for i, value in enumerate(values):
        tile = jnp.where(where == i, value, tile)
    return tile


def split2(value):
    high = value.astype(jnp.bfloat16)
    low = (value - high.astype(F32)).astype(jnp.bfloat16)
    return jnp.concatenate([high, low], axis=-2)


def exchange_kernel(
    n, n_prod, m, slices, loads, wide,
    week_hbm, month_hbm, year_hbm, x_hbm,
    run_out, week_out, month_out, year_out, carry, cross, gains, coef, rollup,
    week, month, year, mixer, x, send1, recv1, send2, half, edges, near, beside, info, far, parts,
    ids_sem, load_sem, ready, i_s, i_r, s1_s, s1_r, s2_s, s2_r, c_s, c_r, f_s, f_r, sib_s, sib_r, near_s, near_r, b_s, b_r,
):
    me = lax.axis_index("date")
    core = lax.axis_index("prod")
    columns, span, lanes = x.shape
    rows = columns // slices
    chunk = columns // loads
    last = span - 1
    upper = me >= m
    lower = me < m
    base = jnp.where(upper, m, 0)
    there = m - base
    here = me - base
    order = sorted(range(1, m), key=lambda d: -min(d, m - d))
    loaded = [
        pltpu.make_async_copy(
            x_hbm.at[pl.ds(i * chunk, chunk)], x.at[pl.ds(i * chunk, chunk)], load_sem.at[i]
        )
        for i in range(loads)
    ]
    fetched = [
        pltpu.make_async_copy(source, target, ids_sem.at[i])
        for i, (source, target) in enumerate(
            ((year_hbm, year), (week_hbm, week), (month_hbm, month))
        )
    ]
    for copy in fetched + loaded:
        copy.start()

    barrier = pltpu.get_barrier_semaphore()

    def greet(date, prod):
        pl.semaphore_signal(barrier, inc=1, device_id=(date, prod), device_id_type=MESH)

    @pl.when(lower)
    def _():
        for j in reversed(range(m)):
            greet(m + j, core)

    for d in order:
        greet(base + lax.rem(here + d, m), core)
    for d in range(1, n_prod):
        greet(me, lax.rem(core + d, n_prod))

    @pl.when(me == m)
    def _():
        greet(m - 1, core)

    for copy in fetched:
        copy.wait()
    head_y, tail_y = edge_masks(year, span, lanes)
    head_w, tail_w = edge_masks(week, span, lanes)
    head_m, tail_m = edge_masks(month, span, lanes)
    lane = lax.broadcasted_iota(jnp.int32, (1, lanes), 1)
    ids = jnp.zeros((1, lanes), F32)
    for i, v in enumerate((year[0], year[last], week[0], week[last], month[0], month[last])):
        ids = jnp.where(lane == i, v.astype(F32), ids)
    wider = 2 * span
    sub = lax.broadcasted_iota(jnp.int32, (span, wider), 0)
    place = lax.broadcasted_iota(jnp.int32, (span, wider), 1) % span
    mixer[0:span] = jnp.where(place <= sub, 1.0, 0.0).astype(mixer.dtype)
    for k, level in enumerate((year, week, month)):
        same = id_column(level, span, wider) == id_row(level, span, wider)
        mixer[(k + 1) * span : (k + 2) * span] = jnp.where(same, 1.0, 0.0).astype(mixer.dtype)

    @pl.when(lower)
    def _():
        for j in range(m):
            cross[j, 0] = jnp.zeros((rows, lanes), F32)

    @pl.when(me == 0)
    def _():
        near[0] = jnp.zeros(near.shape[1:], F32)
        beside[0] = jnp.zeros(beside.shape[1:], F32)

    @pl.when(me == n - 1)
    def _():
        near[1] = jnp.zeros(near.shape[1:], F32)
        beside[1] = jnp.zeros(beside.shape[1:], F32)

    def outer_sums(s, total):
        block = x[pl.ds(pl.multiple_of(s * rows, rows), rows)]
        send1[s, 0] = jnp.sum(block * head_y[None], axis=1)
        send1[s, 1] = jnp.sum(block, axis=1)
        if wide:
            send1[s, 2] = jnp.sum(block * tail_y[None], axis=1)
        return total + jnp.sum(block, axis=0)

    total = jnp.zeros((span, lanes), F32)
    per_load = slices // loads
    for i in range(loads):
        loaded[i].wait()
        total = lax.fori_loop(i * per_load, (i + 1) * per_load, outer_sums, total)
    info[here] = stack_rows(
        [jnp.sum(total, axis=0, keepdims=True)]
        + [
            jnp.sum(total * mask, axis=0, keepdims=True)
            for mask in (head_y, tail_y, head_w, tail_w, head_m, tail_m)
        ]
        + [ids],
        8, lanes,
    )
    recv1[here] = send1[lax.rem(here, slices)]
    pl.semaphore_wait(
        barrier,
        m - 1 + n_prod - 1 + jnp.where(upper, m, 0) + jnp.where(me == m - 1, 1, 0),
    )

    @pl.when(upper)
    def _():
        for j in range(m):
            pl.semaphore_signal(ready, inc=1, device_id=(j, core), device_id_type=MESH)

    def to_mates(source, target, send_sem, recv_sem):
        copies = []
        for d in order:
            peer = lax.rem(here + d, m)
            copy = pltpu.make_async_remote_copy(
                src_ref=source(peer), dst_ref=target.at[here],
                send_sem=send_sem.at[peer], recv_sem=recv_sem.at[here],
                device_id=(base + peer, core), device_id_type=MESH,
            )
            copy.start()
            copies.append(copy)
        return copies

    def from_mates(target, send_sem, recv_sem):
        for d in order:
            peer = lax.rem(here + d, m)
            pltpu.make_async_remote_copy(
                src_ref=target.at[here], dst_ref=target.at[peer],
                send_sem=send_sem.at[peer], recv_sem=recv_sem.at[peer],
                device_id=(base + peer, core), device_id_type=MESH,
            ).wait_recv()

    sent = to_mates(lambda peer: info.at[here], info, i_s, i_r)
    sent += to_mates(lambda peer: send1.at[lax.rem(peer, slices)], recv1, s1_s, s1_r)

    linked = (me < n - 1, me > 0)
    aside = (lax.rem(me + 1, n), lax.rem(me + n - 1, n))

    def edge_copy(side, level):
        return pltpu.make_async_remote_copy(
            src_ref=edges.at[side, level], dst_ref=near.at[side, level],
            send_sem=near_s.at[side, level], recv_sem=near_r.at[side, level],
            device_id=(aside[side], core), device_id_type=MESH,
        )

    def tile_copy(side):
        return pltpu.make_async_remote_copy(
            src_ref=info.at[here], dst_ref=beside.at[side],
            send_sem=b_s.at[side], recv_sem=b_r.at[side],
            device_id=(aside[side], core), device_id_type=MESH,
        )

    for side in range(2):

        @pl.when(linked[side])
        def _():
            tile_copy(side).start()

    def edge_sums(level, head, tail):
        def inner_sums(s, nothing):
            at = pl.ds(pl.multiple_of(s * rows, rows), rows)
            block = x[at]
            edges[0, level, at] = jnp.sum(block * tail[None], axis=1)
            edges[1, level, at] = jnp.sum(block * head[None], axis=1)
            return nothing

        lax.fori_loop(0, slices, inner_sums, 0)

    def edge_send(level):
        for side in range(2):

            @pl.when(linked[side])
            def _():
                edge_copy(side, level).start()

    edge_sums(0, head_w, tail_w)
    edge_send(0)
    edge_sums(1, head_m, tail_m)

    def mixed_pair(c, first):
        parts2 = split2(x[pl.ds(c, 2)])
        both = jnp.concatenate([parts2[0], parts2[1]], axis=1)
        return jnp.dot(
            mixer[first * span : (first + 2) * span], both, preferred_element_type=F32
        )

    def mix_far(g, nothing):
        for r in range(0, 8, 2):
            c = g * 8 + r
            mixed = mixed_pair(c, 0)
            for j in range(2):
                own = mixed[:, j * lanes : (j + 1) * lanes]
                run_out[c + j] = own[0:span]
                year_out[c + j] = own[span:]
        return nothing

    lax.fori_loop(0, columns // 8, mix_far, 0)

    from_mates(info, i_s, i_r)
    low = [jnp.broadcast_to(info[b, 7:8, 0:1], (rows, lanes)) for b in range(m)]
    top = [jnp.broadcast_to(info[b, 7:8, 1:2], (rows, lanes)) for b in range(m)]
    from_mates(recv1, s1_s, s1_r)
    zero = jnp.zeros((rows, lanes), F32)

    def cross_copy(peer, both):
        return pltpu.make_async_remote_copy(
            src_ref=half if both else half.at[pl.ds(1, 1)],
            dst_ref=cross.at[here] if both else cross.at[here, pl.ds(1, 1)],
            send_sem=c_s.at[peer], recv_sem=c_r.at[here],
            device_id=(there + peer, core), device_id_type=MESH,
        )

    @pl.when(upper)
    def _():
        leading = zero
        for b in range(m):
            leading = leading + jnp.where(low[b] == low[0], recv1[b, 0], 0.0)
        half[1] = leading
        for j in range(m):
            cross_copy(j, False).start()

    def tail_of(b):
        if wide:
            return recv1[b, 2]
        return jnp.where(low[b] == top[b], recv1[b, 1], recv1[b, 1] - recv1[b, 0])

    running, into = zero, zero
    brought = []
    for b in range(m):
        send2[b, 0] = running
        brought.append(into)
        if wide:
            send2[b, 1] = into
        if b + 1 < m:
            running = running + recv1[b, 1]
            kept = tail_of(b) + jnp.where(low[b] == top[b], into, 0.0)
            into = jnp.where(top[b] == low[b + 1], kept, 0.0)
    back = zero
    for b in reversed(range(m)):
        one = low[b] == top[b]
        if wide:
            send2[b, 2] = back
        else:
            send2[b, 1] = back + jnp.where(one, brought[b], 0.0)
        if b > 0:
            held = recv1[b, 0] + jnp.where(one, back, 0.0)
            back = jnp.where(top[b - 1] == low[b], held, 0.0)
    sent += to_mates(lambda peer: send2.at[peer], carry, s2_s, s2_r)
    carry[here] = send2[here]

    def group_sum(row, chosen):
        value = jnp.zeros((1, lanes), F32)
        for b in range(m):
            value = value + jnp.where(chosen(b), info[b, row : row + 1], 0.0)
        return value

    always = jnp.zeros((1, lanes), F32) == 0.0
    far[0] = stack_rows(
        [
            group_sum(0, lambda b: always),
            group_sum(1, lambda b: low[b][0:1] == low[0][0:1]),
            group_sum(2, lambda b: top[b][0:1] == top[m - 1][0:1]),
            low[0][0:1], top[m - 1][0:1],
        ],
        8, lanes,
    )
    far_copy = pltpu.make_async_remote_copy(
        src_ref=far.at[0], dst_ref=far.at[1], send_sem=f_s, recv_sem=f_r,
        device_id=(there + here, core), device_id_type=MESH,
    )

    @pl.when(lower)
    def _():
        half[0] = running + recv1[m - 1, 1]
        trailing = zero
        for b in range(m):
            trailing = trailing + jnp.where(top[b] == top[m - 1], tail_of(b), 0.0)
        half[1] = trailing
        pl.semaphore_wait(ready, m)
        for j in reversed(range(m)):
            cross_copy(j, True).start()

    far_copy.start()
    edge_send(1)

    for side in range(2):

        @pl.when(linked[1 - side])
        def _():
            tile_copy(side).wait_recv()

    def gain(side, lane_seen, own):
        value = jnp.broadcast_to(beside[side, 7:8, lane_seen : lane_seen + 1], (1, lanes))
        there_is = me > 0 if side == 0 else me < n - 1
        return jnp.where(jnp.logical_and(value == own.astype(F32), there_is), 1.0, 0.0)

    left_w, right_w = head_w * gain(0, 3, week[0]), tail_w * gain(1, 2, week[last])
    left_m, right_m = head_m * gain(0, 5, month[0]), tail_m * gain(1, 4, month[last])
    first_y = head_y if wide else head_y * jnp.where(year[0] == year[last], 0.0, 1.0)
    gains[0] = first_y
    gains[1] = tail_y

    far_copy.wait_recv()
    low_me = jnp.zeros((1, lanes), F32) + year[0].astype(F32)
    top_me = jnp.zeros((1, lanes), F32) + year[last].astype(F32)
    far_low, far_top = far[1, 3:4], far[1, 4:5]
    before = jnp.where(jnp.logical_and(far_top == low_me, upper), 1.0, 0.0)
    after = jnp.where(jnp.logical_and(far_low == top_me, lower), 1.0, 0.0)
    if not wide:
        after = after + before * jnp.where(low_me == top_me, 1.0, 0.0)
    coef[...] = stack_rows([before, after], 8, lanes)
    run_sum = group_sum(0, lambda b: b < here) + jnp.where(upper, far[1, 0:1], 0.0)
    in_sum = group_sum(
        2, lambda b: jnp.logical_and(top[b][0:1] == low_me, b < here)
    ) + before * far[1, 2:3]
    back_sum = group_sum(1, lambda b: jnp.logical_and(low[b][0:1] == top_me, b > here))
    back_sum = back_sum + jnp.where(
        jnp.logical_and(far_low == top_me, lower), far[1, 1:2], 0.0
    )
    if wide:
        first_sum, last_sum = in_sum, back_sum
    else:
        first_sum = run_sum
        last_sum = back_sum + jnp.where(low_me == top_me, in_sum, 0.0)
    parts[core, 0:8] = stack_rows(
        [
            run_sum, first_sum, last_sum,
            beside[0, 4:5], beside[0, 6:7], beside[1, 3:4], beside[1, 5:6],
        ],
        8, lanes,
    )
    parts[core, 8 : 8 + span] = total
    for d in range(1, n_prod):
        peer = lax.rem(core + d, n_prod)
        copy = pltpu.make_async_remote_copy(
            src_ref=parts.at[core], dst_ref=parts.at[core],
            send_sem=sib_s.at[peer], recv_sem=sib_r.at[core],
            device_id=(me, peer), device_id_type=MESH,
        )
        copy.start()
        sent.append(copy)

    for side in range(2):

        @pl.when(linked[1 - side])
        def _():
            for level in range(2):
                edge_copy(side, level).wait_recv()

    def mix_near(g, nothing):
        base_c = pl.multiple_of(g * 8, 8)
        at = pl.ds(base_c, 8)
        from_left_w, from_left_m = near[0, 0, at], near[0, 1, at]
        from_right_w, from_right_m = near[1, 0, at], near[1, 1, at]
        for r in range(0, 8, 2):
            mixed = mixed_pair(base_c + r, 2)
            for j in range(2):
                q = r + j
                row = slice(q, q + 1)
                own = mixed[:, j * lanes : (j + 1) * lanes]
                week_out[base_c + q] = (
                    own[0:span] + from_left_w[row] * left_w + from_right_w[row] * right_w
                )
                month_out[base_c + q] = (
                    own[span:] + from_left_m[row] * left_m + from_right_m[row] * right_m
                )
        return nothing

    lax.fori_loop(0, columns // 8, mix_near, 0)

    for d in range(1, n_prod):
        peer = lax.rem(core + d, n_prod)
        pltpu.make_async_remote_copy(
            src_ref=parts.at[core], dst_ref=parts.at[peer],
            send_sem=sib_s.at[peer], recv_sem=sib_r.at[peer],
            device_id=(me, peer), device_id_type=MESH,
        ).wait_recv()
    whole = parts[0]
    for i in range(1, n_prod):
        whole = whole + parts[i]
    mixed = jnp.dot(mixer[...], split2(whole[8 : 8 + span]), preferred_element_type=F32)
    rollup[0] = mixed[0:span] + whole[0:1]
    rollup[3] = mixed[span : 2 * span] + whole[1:2] * first_y + whole[2:3] * tail_y
    rollup[1] = mixed[2 * span : 3 * span] + whole[3:4] * left_w + whole[5:6] * right_w
    rollup[2] = mixed[3 * span : 4 * span] + whole[4:5] * left_m + whole[6:7] * right_m

    for copy in sent:
        copy.wait_send()
    far_copy.wait_send()
    for side in range(2):

        @pl.when(linked[side])
        def _():
            tile_copy(side).wait_send()
            for level in range(2):
                edge_copy(side, level).wait_send()

    def cross_done(both):
        for j in range(m):
            cross_copy(j, both).wait_send()
        for j in range(m):
            pltpu.make_async_remote_copy(
                src_ref=half.at[pl.ds(1, 1)] if both else half,
                dst_ref=cross.at[j, pl.ds(1, 1)] if both else cross.at[j],
                send_sem=c_s.at[j], recv_sem=c_r.at[j],
                device_id=(there + j, core), device_id_type=MESH,
            ).wait_recv()

    from_mates(carry, s2_s, s2_r)

    @pl.when(lower)
    def _():
        cross_done(True)

    @pl.when(upper)
    def _():
        cross_done(False)


def exchange(n, n_prod, m, slices, wide, week, month, year, sales):
    columns, span, lanes = sales.shape
    rows = columns // slices
    loads = 4 if slices % 4 == 0 else 1
    hbm = pl.BlockSpec(memory_space=pltpu.HBM)
    vmem = pl.BlockSpec(memory_space=pltpu.VMEM)
    packet = (m, 3 if wide else 2, rows, lanes)
    dma = pltpu.SemaphoreType.DMA
    cube = pltpu.VMEM(sales.shape, F32)
    return pl.pallas_call(
        functools.partial(exchange_kernel, n, n_prod, m, slices, loads, wide),
        out_shape=(
            cube, cube, cube, cube,
            pltpu.VMEM(packet, F32),
            pltpu.VMEM((m, 2, rows, lanes), F32),
            pltpu.VMEM((2, span, lanes), F32),
            pltpu.VMEM((8, lanes), F32),
            pltpu.VMEM((4, span, lanes), F32),
        ),
        in_specs=[hbm] * 4,
        out_specs=(vmem,) * 9,
        scratch_shapes=[
            pltpu.SMEM((span,), jnp.int32),
            pltpu.SMEM((span,), jnp.int32),
            pltpu.SMEM((span,), jnp.int32),
            pltpu.VMEM((4 * span, 2 * span), jnp.bfloat16),
            pltpu.VMEM(sales.shape, F32),
            pltpu.VMEM((slices,) + packet[1:], F32),
            pltpu.VMEM(packet, F32),
            pltpu.VMEM(packet, F32),
            pltpu.VMEM((2, rows, lanes), F32),
            pltpu.VMEM((2, 2, columns, lanes), F32),
            pltpu.VMEM((2, 2, columns, lanes), F32),
            pltpu.VMEM((2, 8, lanes), F32),
            pltpu.VMEM((m, 8, lanes), F32),
            pltpu.VMEM((2, 8, lanes), F32),
            pltpu.VMEM((n_prod, 8 + span, lanes), F32),
            dma((3,)), dma((loads,)), pltpu.SemaphoreType.REGULAR,
            dma((m,)), dma((m,)), dma((m,)), dma((m,)), dma((m,)), dma((m,)), dma((m,)), dma((m,)),
            dma, dma, dma((n_prod,)), dma((n_prod,)), dma((2, 2)), dma((2, 2)), dma((2,)), dma((2,)),
        ],
        compiler_params=pltpu.CompilerParams(
            collective_id=0, has_side_effects=True, vmem_limit_bytes=55 << 20
        ),
        name="exchange",
    )(week, month, year, sales)


def apply_kernel(
    wide, slices, steps,
    run_in, week_in, month_in, year_in, carry, cross, gains, coef, rollup_in,
    run_hbm, week_hbm, month_hbm, year_hbm, rollup_hbm,
    run_out, year_out, out_sem, whole_sem,
):
    columns, span, lanes = run_in.shape
    rows = columns // slices
    per_step = slices // steps
    block = columns // steps
    stores = [
        pltpu.make_async_copy(source, target, whole_sem.at[i])
        for i, (source, target) in enumerate(
            ((week_in, week_hbm), (month_in, month_hbm), (rollup_in, rollup_hbm))
        )
    ]
    for copy in stores:
        copy.start()

    def group(g, nothing):
        start = carry[g, 0] + cross[g, 0]
        if wide:
            first = carry[g, 1] + coef[0:1] * cross[g, 1]
            final = carry[g, 2] + coef[1:2] * cross[g, 1]
        else:
            first = start
            final = carry[g, 1] + coef[1:2] * cross[g, 1]
        for r in range(rows):
            c = g * rows + r
            row = slice(r, r + 1)
            run_out[c] = run_in[c] + start[row]
            year_out[c] = year_in[c] + first[row] * gains[0] + final[row] * gains[1]
        return nothing

    for i in range(steps):
        lax.fori_loop(i * per_step, (i + 1) * per_step, group, 0)
        at = pl.ds(i * block, block)
        for k, (source, target) in enumerate(((run_out, run_hbm), (year_out, year_hbm))):
            copy = pltpu.make_async_copy(source.at[at], target.at[at], out_sem.at[i, k])
            copy.start()
            stores.append(copy)
    for copy in stores:
        copy.wait()


def apply(slices, wide, shape, *passed):
    columns, span, lanes = shape
    steps = 8 if slices % 8 == 0 else 1
    hbm = pl.BlockSpec(memory_space=pltpu.HBM)
    vmem = pl.BlockSpec(memory_space=pltpu.VMEM)
    cube_shape = jax.ShapeDtypeStruct(shape, F32)
    cube = pltpu.VMEM(shape, F32)
    dma = pltpu.SemaphoreType.DMA
    return pl.pallas_call(
        functools.partial(apply_kernel, wide, slices, steps),
        out_shape=(cube_shape,) * 4 + (jax.ShapeDtypeStruct((4, span, lanes), F32),),
        in_specs=[vmem] * 9,
        out_specs=(hbm,) * 5,
        scratch_shapes=[cube, cube, dma((steps, 2)), dma((3,))],
        compiler_params=pltpu.CompilerParams(vmem_limit_bytes=16 << 20),
        name="apply",
    )(*passed)


def solution(mesh):
    n, n_prod = mesh.shape["date"], mesh.shape["prod"]

    def local(sales, week, month, year):
        m = n // 2
        slices = min(m, sales.shape[0] // 8)
        wide = n * sales.shape[1] // 300 + 1 > 2
        passed = exchange(n, n_prod, m, slices, wide, week, month, year, sales)
        return apply(slices, wide, sales.shape, *passed)

    return jax.shard_map(
        local,
        mesh=mesh,
        in_specs=(P("prod", "date", None), P("date"), P("date"), P("date")),
        out_specs=(P("prod", "date", None),) * 4 + (P(None, "date", None),),
        check_vma=False,
    )
```

time: 26.2 us -> 24 us (0.916); the launches traced: 26 us -> 23.5 us
  Pallas kernels: 25.4 us -> 22.9 us
    pallas_call x2, Pallas kernels: 25.4 us -> 22.9 us  [the longest x1 19.4 us: exchange(): pl.pallas_call(functools.partial(exchange_kernel, n, n_prod, m, slices, l...]
where the time goes in v1:
time: 24 us; the launch traced here: 23.5 us
  Pallas kernels  22.9 us (95%)
  between operations  0.64 us (3%)
    pallas_call x1, Pallas kernels, exchange(): pl.pallas_call(functools.partial(exchange_kernel, n, n_prod, m, slices, l...  19.4 us
    pallas_call x1, Pallas kernels, apply(): pl.pallas_call(functools.partial(apply_kernel, wide, slices, steps), out_...  3.49 us

profile of v1, /device:TPU:0, one launch (start us, length us, event | category | flops | bytes accessed | tf_op | source)
XLA Modules:
  0.0 23.5 jit_solution(2976007281233895457)
XLA Ops:
  0.6 19.4 %exchange.1 = (f32[128,32,128]{2,1,0:T(8,128)S(1)}, f32[128,32,128]{2,1,0:T(8,128)S(1)}, f32[128,32,128]{2,1,0:T(8,128)S(1)}, f32[128,32,128]{2,1,0:T(8,128)S(1)...) custom-call(s32[32]{0:T(128)} %week_hbm.1, ...), custom_call_target="tpu_custom_call" | custom-call | tf_op jit(solution)/shard_map/exchange/pallas_call | solution.py:485
  20.1 3.5 %apply.1 = (f32[128,32,128]{2,1,0:T(8,128)}, f32[128,32,128]{2,1,0:T(8,128)}, f32[128,32,128]{2,1,0:T(8,128)}, f32[128,32,128]{2,1,0:T(8,128)}, f32[4,32,128]{2,1,0:T(8,128)}) custom-call(f32[128,32,128]{2,1,0:T(8,128)S(1)} %get-tuple-element.14.run_in, f32[128,32,128]{2,1,0:T(8,128)S(1)} %get-tuple-element.15.week_in, ...), custom_call_target="tpu_custom_call" | custom-call | tf_op jit(solution)/shard_map/apply/pallas_call | solution.py:577

commit v2 on v1

--- a/solution.py
+++ b/solution.py
@@ -49,8 +49,8 @@
 def exchange_kernel(
     n, n_prod, m, slices, loads, wide,
     week_hbm, month_hbm, year_hbm, x_hbm,
-    run_out, week_out, month_out, year_out, carry, cross, gains, coef, rollup,
-    week, month, year, mixer, x, send1, recv1, send2, half, edges, near, beside, info, far, parts,
+    run_out, week_out, month_out, year_out, carry, cross, near_m, gains, coef, rollup,
+    week, month, year, mixer, x, send1, recv1, send2, half, edges, near_w, beside, info, far, parts,
     ids_sem, load_sem, ready, i_s, i_r, s1_s, s1_r, s2_s, s2_r, c_s, c_r, f_s, f_r, sib_s, sib_r, near_s, near_r, b_s, b_r,
 ):
     me = lax.axis_index("date")
@@ -108,29 +108,6 @@
     ids = jnp.zeros((1, lanes), F32)
     for i, v in enumerate((year[0], year[last], week[0], week[last], month[0], month[last])):
         ids = jnp.where(lane == i, v.astype(F32), ids)
-    wider = 2 * span
-    sub = lax.broadcasted_iota(jnp.int32, (span, wider), 0)
-    place = lax.broadcasted_iota(jnp.int32, (span, wider), 1) % span
-    mixer[0:span] = jnp.where(place <= sub, 1.0, 0.0).astype(mixer.dtype)
-    for k, level in enumerate((year, week, month)):
-        same = id_column(level, span, wider) == id_row(level, span, wider)
-        mixer[(k + 1) * span : (k + 2) * span] = jnp.where(same, 1.0, 0.0).astype(mixer.dtype)
-
-    @pl.when(lower)
-    def _():
-        for j in range(m):
-            cross[j, 0] = jnp.zeros((rows, lanes), F32)
-
-    @pl.when(me == 0)
-    def _():
-        near[0] = jnp.zeros(near.shape[1:], F32)
-        beside[0] = jnp.zeros(beside.shape[1:], F32)
-
-    @pl.when(me == n - 1)
-    def _():
-        near[1] = jnp.zeros(near.shape[1:], F32)
-        beside[1] = jnp.zeros(beside.shape[1:], F32)
-
     def outer_sums(s, total):
         block = x[pl.ds(pl.multiple_of(s * rows, rows), rows)]
         send1[s, 0] = jnp.sum(block * head_y[None], axis=1)
@@ -194,7 +171,7 @@
 
     def edge_copy(side, level):
         return pltpu.make_async_remote_copy(
-            src_ref=edges.at[side, level], dst_ref=near.at[side, level],
+            src_ref=edges.at[side, level], dst_ref=(near_w, near_m)[level].at[side],
             send_sem=near_s.at[side, level], recv_sem=near_r.at[side, level],
             device_id=(aside[side], core), device_id_type=MESH,
         )
@@ -211,6 +188,23 @@
         @pl.when(linked[side])
         def _():
             tile_copy(side).start()
+
+    @pl.when(lower)
+    def _():
+        for j in range(m):
+            cross[j, 0] = jnp.zeros((rows, lanes), F32)
+
+    @pl.when(me == 0)
+    def _():
+        near_w[0] = jnp.zeros(near_w.shape[1:], F32)
+        near_m[0] = jnp.zeros(near_m.shape[1:], F32)
+        beside[0] = jnp.zeros(beside.shape[1:], F32)
+
+    @pl.when(me == n - 1)
+    def _():
+        near_w[1] = jnp.zeros(near_w.shape[1:], F32)
+        near_m[1] = jnp.zeros(near_m.shape[1:], F32)
+        beside[1] = jnp.zeros(beside.shape[1:], F32)
 
     def edge_sums(level, head, tail):
         def inner_sums(s, nothing):
@@ -232,6 +226,14 @@
     edge_sums(0, head_w, tail_w)
     edge_send(0)
     edge_sums(1, head_m, tail_m)
+    wider = 2 * span
+    sub = lax.broadcasted_iota(jnp.int32, (span, wider), 0)
+    place = lax.broadcasted_iota(jnp.int32, (span, wider), 1) % span
+    mixer[0:span] = jnp.where(place <= sub, 1.0, 0.0).astype(mixer.dtype)
+    for k, level in enumerate((year, week, month)):
+        same = id_column(level, span, wider) == id_row(level, span, wider)
+        mixer[(k + 1) * span : (k + 2) * span] = jnp.where(same, 1.0, 0.0).astype(mixer.dtype)
+
 
     def mixed_pair(c, first):
         parts2 = split2(x[pl.ds(c, 2)])
@@ -240,9 +242,11 @@
             mixer[first * span : (first + 2) * span], both, preferred_element_type=F32
         )
 
+    stride = min(columns, 32)
+
     def mix_far(g, nothing):
-        for r in range(0, 8, 2):
-            c = g * 8 + r
+        for r in range(0, stride, 2):
+            c = g * stride + r
             mixed = mixed_pair(c, 0)
             for j in range(2):
                 own = mixed[:, j * lanes : (j + 1) * lanes]
@@ -250,7 +254,7 @@
                 year_out[c + j] = own[span:]
         return nothing
 
-    lax.fori_loop(0, columns // 8, mix_far, 0)
+    lax.fori_loop(0, columns // stride, mix_far, 0)
 
     from_mates(info, i_s, i_r)
     low = [jnp.broadcast_to(info[b, 7:8, 0:1], (rows, lanes)) for b in range(m)]
@@ -355,6 +359,27 @@
     first_y = head_y if wide else head_y * jnp.where(year[0] == year[last], 0.0, 1.0)
     gains[0] = first_y
     gains[1] = tail_y
+    gains[2] = left_m
+    gains[3] = right_m
+
+    for side in range(2):
+
+        @pl.when(linked[1 - side])
+        def _():
+            edge_copy(side, 0).wait_recv()
+
+    def mix_near(g, nothing):
+        for r in range(0, stride, 2):
+            mixed = mixed_pair(g * stride + r, 2)
+            for j in range(2):
+                c = g * stride + r + j
+                row = pl.ds(c, 1)
+                own = mixed[:, j * lanes : (j + 1) * lanes]
+                week_out[c] = own[0:span] + near_w[0, row] * left_w + near_w[1, row] * right_w
+                month_out[c] = own[span:]
+        return nothing
+
+    lax.fori_loop(0, columns // stride, mix_near, 0)
 
     far_copy.wait_recv()
     low_me = jnp.zeros((1, lanes), F32) + year[0].astype(F32)
@@ -396,34 +421,6 @@
         copy.start()
         sent.append(copy)
 
-    for side in range(2):
-
-        @pl.when(linked[1 - side])
-        def _():
-            for level in range(2):
-                edge_copy(side, level).wait_recv()
-
-    def mix_near(g, nothing):
-        base_c = pl.multiple_of(g * 8, 8)
-        at = pl.ds(base_c, 8)
-        from_left_w, from_left_m = near[0, 0, at], near[0, 1, at]
-        from_right_w, from_right_m = near[1, 0, at], near[1, 1, at]
-        for r in range(0, 8, 2):
-            mixed = mixed_pair(base_c + r, 2)
-            for j in range(2):
-                q = r + j
-                row = slice(q, q + 1)
-                own = mixed[:, j * lanes : (j + 1) * lanes]
-                week_out[base_c + q] = (
-                    own[0:span] + from_left_w[row] * left_w + from_right_w[row] * right_w
-                )
-                month_out[base_c + q] = (
-                    own[span:] + from_left_m[row] * left_m + from_right_m[row] * right_m
-                )
-        return nothing
-
-    lax.fori_loop(0, columns // 8, mix_near, 0)
-
     for d in range(1, n_prod):
         peer = lax.rem(core + d, n_prod)
         pltpu.make_async_remote_copy(
@@ -462,6 +459,12 @@
                 device_id=(there + j, core), device_id_type=MESH,
             ).wait_recv()
 
+    for side in range(2):
+
+        @pl.when(linked[1 - side])
+        def _():
+            edge_copy(side, 1).wait_recv()
+
     from_mates(carry, s2_s, s2_r)
 
     @pl.when(lower)
@@ -488,12 +491,13 @@
             cube, cube, cube, cube,
             pltpu.VMEM(packet, F32),
             pltpu.VMEM((m, 2, rows, lanes), F32),
-            pltpu.VMEM((2, span, lanes), F32),
+            pltpu.VMEM((2, columns, lanes), F32),
+            pltpu.VMEM((4, span, lanes), F32),
             pltpu.VMEM((8, lanes), F32),
             pltpu.VMEM((4, span, lanes), F32),
         ),
         in_specs=[hbm] * 4,
-        out_specs=(vmem,) * 9,
+        out_specs=(vmem,) * 10,
         scratch_shapes=[
             pltpu.SMEM((span,), jnp.int32),
             pltpu.SMEM((span,), jnp.int32),
@@ -505,7 +509,7 @@
             pltpu.VMEM(packet, F32),
             pltpu.VMEM((2, rows, lanes), F32),
             pltpu.VMEM((2, 2, columns, lanes), F32),
-            pltpu.VMEM((2, 2, columns, lanes), F32),
+            pltpu.VMEM((2, columns, lanes), F32),
             pltpu.VMEM((2, 8, lanes), F32),
             pltpu.VMEM((m, 8, lanes), F32),
             pltpu.VMEM((2, 8, lanes), F32),
@@ -523,9 +527,9 @@
 
 def apply_kernel(
     wide, slices, steps,
-    run_in, week_in, month_in, year_in, carry, cross, gains, coef, rollup_in,
+    run_in, week_in, month_in, year_in, carry, cross, near_m, gains, coef, rollup_in,
     run_hbm, week_hbm, month_hbm, year_hbm, rollup_hbm,
-    run_out, year_out, out_sem, whole_sem,
+    run_out, month_out, year_out, out_sem, whole_sem,
 ):
     columns, span, lanes = run_in.shape
     rows = columns // slices
@@ -534,7 +538,7 @@
     stores = [
         pltpu.make_async_copy(source, target, whole_sem.at[i])
         for i, (source, target) in enumerate(
-            ((week_in, week_hbm), (month_in, month_hbm), (rollup_in, rollup_hbm))
+            ((week_in, week_hbm), (rollup_in, rollup_hbm))
         )
     ]
     for copy in stores:
@@ -551,14 +555,18 @@
         for r in range(rows):
             c = g * rows + r
             row = slice(r, r + 1)
+            side = pl.ds(c, 1)
             run_out[c] = run_in[c] + start[row]
+            month_out[c] = month_in[c] + near_m[0, side] * gains[2] + near_m[1, side] * gains[3]
             year_out[c] = year_in[c] + first[row] * gains[0] + final[row] * gains[1]
         return nothing
 
     for i in range(steps):
         lax.fori_loop(i * per_step, (i + 1) * per_step, group, 0)
         at = pl.ds(i * block, block)
-        for k, (source, target) in enumerate(((run_out, run_hbm), (year_out, year_hbm))):
+        for k, (source, target) in enumerate(
+            ((run_out, run_hbm), (month_out, month_hbm), (year_out, year_hbm))
+        ):
             copy = pltpu.make_async_copy(source.at[at], target.at[at], out_sem.at[i, k])
             copy.start()
             stores.append(copy)
@@ -577,9 +585,9 @@
     return pl.pallas_call(
         functools.partial(apply_kernel, wide, slices, steps),
         out_shape=(cube_shape,) * 4 + (jax.ShapeDtypeStruct((4, span, lanes), F32),),
-        in_specs=[vmem] * 9,
+        in_specs=[vmem] * 10,
         out_specs=(hbm,) * 5,
-        scratch_shapes=[cube, cube, dma((steps, 2)), dma((3,))],
+        scratch_shapes=[cube, cube, cube, dma((steps, 3)), dma((2,))],
         compiler_params=pltpu.CompilerParams(vmem_limit_bytes=16 << 20),
         name="apply",
     )(*passed)

time: 24 us -> 20.9 us (0.87); the launches traced: 23.5 us -> 20.7 us
  Pallas kernels: 22.9 us -> 20.1 us
    pallas_call x1, Pallas kernels: 19.4 us -> 16.5 us  [exchange(): pl.pallas_call(functools.partial(exchange_kernel, n, n_prod, m, slices, l...]
where the time goes in v2:
time: 20.9 us; the launch traced here: 20.7 us
  Pallas kernels  20.1 us (96%)
  between operations  0.64 us (3%)
    pallas_call x1, Pallas kernels, exchange(): pl.pallas_call(functools.partial(exchange_kernel, n, n_prod, m, slices, l...  16.5 us
    pallas_call x1, Pallas kernels, apply(): pl.pallas_call(functools.partial(apply_kernel, wide, slices, steps), out_...  3.58 us

profile of v2, /device:TPU:0, one launch (start us, length us, event | category | flops | bytes accessed | tf_op | source)
XLA Modules:
  0.0 20.7 jit_solution(4196012913358415984)
XLA Ops:
  0.6 16.5 %exchange.1 = (f32[128,32,128]{2,1,0:T(8,128)S(1)}, f32[128,32,128]{2,1,0:T(8,128)S(1)}, f32[128,32,128]{2,1,0:T(8,128)S(1)}, f32[128,32,128]{2,1,0:T(8,128)S(1)...) custom-call(s32[32]{0:T(128)} %week_hbm.1, ...), custom_call_target="tpu_custom_call" | custom-call | tf_op jit(solution)/shard_map/exchange/pallas_call | solution.py:488
  17.1 3.6 %apply.1 = (f32[128,32,128]{2,1,0:T(8,128)}, f32[128,32,128]{2,1,0:T(8,128)}, f32[128,32,128]{2,1,0:T(8,128)}, f32[128,32,128]{2,1,0:T(8,128)}, f32[4,32,128]{2,1,0:T(8,128)}) custom-call(f32[128,32,128]{2,1,0:T(8,128)S(1)} %get-tuple-element.15.run_in, f32[128,32,128]{2,1,0:T(8,128)S(1)} %get-tuple-element.16.week_in, ...), custom_call_target="tpu_custom_call" | custom-call | tf_op jit(solution)/shard_map/apply/pallas_call | solution.py:585

commit v3 on v2

--- a/solution.py
+++ b/solution.py
@@ -49,8 +49,8 @@
 def exchange_kernel(
     n, n_prod, m, slices, loads, wide,
     week_hbm, month_hbm, year_hbm, x_hbm,
-    run_out, week_out, month_out, year_out, carry, cross, near_m, gains, coef, rollup,
-    week, month, year, mixer, x, send1, recv1, send2, half, edges, near_w, beside, info, far, parts,
+    run_out, week_out, month_out, year_out, carry, cross, near_m, gains, own, far, rollup,
+    week, month, year, mixer, x, send1, recv1, send2, half, edges, near_w, beside, info, group, parts,
     ids_sem, load_sem, ready, i_s, i_r, s1_s, s1_r, s2_s, s2_r, c_s, c_r, f_s, f_r, sib_s, sib_r, near_s, near_r, b_s, b_r,
 ):
     me = lax.axis_index("date")
@@ -64,6 +64,8 @@
     base = jnp.where(upper, m, 0)
     there = m - base
     here = me - base
+    nearer = (m + 1) // 2
+    farther = jnp.where(here >= nearer, 1, 0)
     order = sorted(range(1, m), key=lambda d: -min(d, m - d))
     loaded = [
         pltpu.make_async_copy(
@@ -89,6 +91,8 @@
     def _():
         for j in reversed(range(m)):
             greet(m + j, core)
+        for d in range(1, n_prod):
+            greet(m + here, lax.rem(core + d, n_prod))
 
     for d in order:
         greet(base + lax.rem(here + d, m), core)
@@ -133,13 +137,20 @@
     recv1[here] = send1[lax.rem(here, slices)]
     pl.semaphore_wait(
         barrier,
-        m - 1 + n_prod - 1 + jnp.where(upper, m, 0) + jnp.where(me == m - 1, 1, 0),
+        m - 1 + n_prod - 1 + jnp.where(upper, m + n_prod - 1, 0) + jnp.where(me == m - 1, 1, 0),
     )
 
     @pl.when(upper)
     def _():
         for j in range(m):
-            pl.semaphore_signal(ready, inc=1, device_id=(j, core), device_id_type=MESH)
+            pl.semaphore_signal(
+                ready.at[farther], inc=1, device_id=(j, core), device_id_type=MESH
+            )
+        for d in range(1, n_prod):
+            pl.semaphore_signal(
+                ready.at[1], inc=1, device_id=(here, lax.rem(core + d, n_prod)),
+                device_id_type=MESH,
+            )
 
     def to_mates(source, target, send_sem, recv_sem):
         copies = []
@@ -220,6 +231,13 @@
         for side in range(2):
 
             @pl.when(linked[side])
+            def _():
+                edge_copy(side, level).start()
+
+    def edge_send_where(level, where):
+        for side in range(2):
+
+            @pl.when(jnp.logical_and(linked[side], where))
             def _():
                 edge_copy(side, level).start()
 
@@ -306,6 +324,7 @@
             held = recv1[b, 0] + jnp.where(one, back, 0.0)
             back = jnp.where(top[b - 1] == low[b], held, 0.0)
     sent += to_mates(lambda peer: send2.at[peer], carry, s2_s, s2_r)
+    edge_send_where(1, me == m - 1)
     carry[here] = send2[here]
 
     def group_sum(row, chosen):
@@ -315,7 +334,7 @@
         return value
 
     always = jnp.zeros((1, lanes), F32) == 0.0
-    far[0] = stack_rows(
+    group[...] = stack_rows(
         [
             group_sum(0, lambda b: always),
             group_sum(1, lambda b: low[b][0:1] == low[0][0:1]),
@@ -324,10 +343,20 @@
         ],
         8, lanes,
     )
-    far_copy = pltpu.make_async_remote_copy(
-        src_ref=far.at[0], dst_ref=far.at[1], send_sem=f_s, recv_sem=f_r,
-        device_id=(there + here, core), device_id_type=MESH,
-    )
+    def far_copy(prod):
+        return pltpu.make_async_remote_copy(
+            src_ref=group, dst_ref=far.at[core], send_sem=f_s.at[prod], recv_sem=f_r.at[core],
+            device_id=(there + here, prod), device_id_type=MESH,
+        )
+
+    def far_send():
+        for prod in range(n_prod):
+            far_copy(prod).start()
+
+    @pl.when(upper)
+    def _():
+        far_send()
+
 
     @pl.when(lower)
     def _():
@@ -336,12 +365,13 @@
         for b in range(m):
             trailing = trailing + jnp.where(top[b] == top[m - 1], tail_of(b), 0.0)
         half[1] = trailing
-        pl.semaphore_wait(ready, m)
+        pl.semaphore_wait(ready.at[0], nearer)
+        pl.semaphore_wait(ready.at[1], m - nearer + n_prod - 1)
         for j in reversed(range(m)):
             cross_copy(j, True).start()
-
-    far_copy.start()
-    edge_send(1)
+        far_send()
+
+    edge_send_where(1, me != m - 1)
 
     for side in range(2):
 
@@ -381,31 +411,17 @@
 
     lax.fori_loop(0, columns // stride, mix_near, 0)
 
-    far_copy.wait_recv()
     low_me = jnp.zeros((1, lanes), F32) + year[0].astype(F32)
     top_me = jnp.zeros((1, lanes), F32) + year[last].astype(F32)
-    far_low, far_top = far[1, 3:4], far[1, 4:5]
-    before = jnp.where(jnp.logical_and(far_top == low_me, upper), 1.0, 0.0)
-    after = jnp.where(jnp.logical_and(far_low == top_me, lower), 1.0, 0.0)
+    one_me = jnp.where(low_me == top_me, 1.0, 0.0)
+    run_sum = group_sum(0, lambda b: b < here)
+    in_sum = group_sum(2, lambda b: jnp.logical_and(top[b][0:1] == low_me, b < here))
+    back_sum = group_sum(1, lambda b: jnp.logical_and(low[b][0:1] == top_me, b > here))
     if not wide:
-        after = after + before * jnp.where(low_me == top_me, 1.0, 0.0)
-    coef[...] = stack_rows([before, after], 8, lanes)
-    run_sum = group_sum(0, lambda b: b < here) + jnp.where(upper, far[1, 0:1], 0.0)
-    in_sum = group_sum(
-        2, lambda b: jnp.logical_and(top[b][0:1] == low_me, b < here)
-    ) + before * far[1, 2:3]
-    back_sum = group_sum(1, lambda b: jnp.logical_and(low[b][0:1] == top_me, b > here))
-    back_sum = back_sum + jnp.where(
-        jnp.logical_and(far_low == top_me, lower), far[1, 1:2], 0.0
-    )
-    if wide:
-        first_sum, last_sum = in_sum, back_sum
-    else:
-        first_sum = run_sum
-        last_sum = back_sum + jnp.where(low_me == top_me, in_sum, 0.0)
+        back_sum = back_sum + one_me * in_sum
     parts[core, 0:8] = stack_rows(
         [
-            run_sum, first_sum, last_sum,
+            run_sum, in_sum, back_sum,
             beside[0, 4:5], beside[0, 6:7], beside[1, 3:4], beside[1, 5:6],
         ],
         8, lanes,
@@ -432,14 +448,22 @@
     for i in range(1, n_prod):
         whole = whole + parts[i]
     mixed = jnp.dot(mixer[...], split2(whole[8 : 8 + span]), preferred_element_type=F32)
-    rollup[0] = mixed[0:span] + whole[0:1]
-    rollup[3] = mixed[span : 2 * span] + whole[1:2] * first_y + whole[2:3] * tail_y
+    rollup[0] = mixed[0:span]
+    rollup[3] = mixed[span : 2 * span]
     rollup[1] = mixed[2 * span : 3 * span] + whole[3:4] * left_w + whole[5:6] * right_w
     rollup[2] = mixed[3 * span : 4 * span] + whole[4:5] * left_m + whole[6:7] * right_m
+    own[...] = stack_rows(
+        [
+            whole[0:1], whole[1:2], whole[2:3], low_me, top_me, one_me,
+            jnp.zeros((1, lanes), F32) + jnp.where(upper, 1.0, 0.0),
+        ],
+        8, lanes,
+    )
 
     for copy in sent:
         copy.wait_send()
-    far_copy.wait_send()
+    for prod in range(n_prod):
+        far_copy(prod).wait_send()
     for side in range(2):
 
         @pl.when(linked[side])
@@ -465,6 +489,11 @@
         def _():
             edge_copy(side, 1).wait_recv()
 
+    for prod in range(n_prod):
+        pltpu.make_async_remote_copy(
+            src_ref=group, dst_ref=far.at[prod], send_sem=f_s.at[prod], recv_sem=f_r.at[prod],
+            device_id=(there + here, prod), device_id_type=MESH,
+        ).wait_recv()
     from_mates(carry, s2_s, s2_r)
 
     @pl.when(lower)
@@ -494,10 +523,11 @@
             pltpu.VMEM((2, columns, lanes), F32),
             pltpu.VMEM((4, span, lanes), F32),
             pltpu.VMEM((8, lanes), F32),
+            pltpu.VMEM((n_prod, 8, lanes), F32),
             pltpu.VMEM((4, span, lanes), F32),
         ),
         in_specs=[hbm] * 4,
-        out_specs=(vmem,) * 10,
+        out_specs=(vmem,) * 11,
         scratch_shapes=[
             pltpu.SMEM((span,), jnp.int32),
             pltpu.SMEM((span,), jnp.int32),
@@ -512,11 +542,11 @@
             pltpu.VMEM((2, columns, lanes), F32),
             pltpu.VMEM((2, 8, lanes), F32),
             pltpu.VMEM((m, 8, lanes), F32),
-            pltpu.VMEM((2, 8, lanes), F32),
+            pltpu.VMEM((8, lanes), F32),
             pltpu.VMEM((n_prod, 8 + span, lanes), F32),
-            dma((3,)), dma((loads,)), pltpu.SemaphoreType.REGULAR,
+            dma((3,)), dma((loads,)), pltpu.SemaphoreType.REGULAR((2,)),
             dma((m,)), dma((m,)), dma((m,)), dma((m,)), dma((m,)), dma((m,)), dma((m,)), dma((m,)),
-            dma, dma, dma((n_prod,)), dma((n_prod,)), dma((2, 2)), dma((2, 2)), dma((2,)), dma((2,)),
+            dma((n_prod,)), dma((n_prod,)), dma((n_prod,)), dma((n_prod,)), dma((2, 2)), dma((2, 2)), dma((2,)), dma((2,)),
         ],
         compiler_params=pltpu.CompilerParams(
             collective_id=0, has_side_effects=True, vmem_limit_bytes=55 << 20
@@ -527,31 +557,45 @@
 
 def apply_kernel(
     wide, slices, steps,
-    run_in, week_in, month_in, year_in, carry, cross, near_m, gains, coef, rollup_in,
+    run_in, week_in, month_in, year_in, carry, cross, near_m, gains, own, far, rollup_in,
     run_hbm, week_hbm, month_hbm, year_hbm, rollup_hbm,
-    run_out, month_out, year_out, out_sem, whole_sem,
+    run_out, month_out, year_out, rollup, out_sem, whole_sem,
 ):
     columns, span, lanes = run_in.shape
     rows = columns // slices
     per_step = slices // steps
     block = columns // steps
-    stores = [
-        pltpu.make_async_copy(source, target, whole_sem.at[i])
-        for i, (source, target) in enumerate(
-            ((week_in, week_hbm), (rollup_in, rollup_hbm))
-        )
-    ]
-    for copy in stores:
-        copy.start()
+    stores = [pltpu.make_async_copy(week_in, week_hbm, whole_sem.at[0])]
+    stores[0].start()
+    low_me, top_me, one_me, above = own[3:4], own[4:5], own[5:6], own[6:7]
+    before = jnp.where(far[0, 4:5] == low_me, above, 0.0)
+    after = jnp.where(far[0, 3:4] == top_me, 1.0 - above, 0.0)
+    beyond = far[0]
+    for prod in range(1, far.shape[0]):
+        beyond = beyond + far[prod]
+    run_sum = own[0:1] + above * beyond[0:1]
+    in_sum = before * beyond[2:3]
+    back_sum = own[2:3] + after * beyond[1:2]
+    if wide:
+        first_sum, last_sum = own[1:2] + in_sum, back_sum
+    else:
+        first_sum, last_sum = run_sum, back_sum + one_me * in_sum
+        after = after + before * one_me
+    rollup[0] = rollup_in[0] + run_sum
+    rollup[1] = rollup_in[1]
+    rollup[2] = rollup_in[2]
+    rollup[3] = rollup_in[3] + first_sum * gains[0] + last_sum * gains[1]
+    stores.append(pltpu.make_async_copy(rollup, rollup_hbm, whole_sem.at[1]))
+    stores[1].start()
 
     def group(g, nothing):
         start = carry[g, 0] + cross[g, 0]
         if wide:
-            first = carry[g, 1] + coef[0:1] * cross[g, 1]
-            final = carry[g, 2] + coef[1:2] * cross[g, 1]
+            first = carry[g, 1] + before * cross[g, 1]
+            final = carry[g, 2] + after * cross[g, 1]
         else:
             first = start
-            final = carry[g, 1] + coef[1:2] * cross[g, 1]
+            final = carry[g, 1] + after * cross[g, 1]
         for r in range(rows):
             c = g * rows + r
             row = slice(r, r + 1)
@@ -576,7 +620,7 @@
 
 def apply(slices, wide, shape, *passed):
     columns, span, lanes = shape
-    steps = 8 if slices % 8 == 0 else 1
+    steps = 4 if slices % 4 == 0 else 1
     hbm = pl.BlockSpec(memory_space=pltpu.HBM)
     vmem = pl.BlockSpec(memory_space=pltpu.VMEM)
     cube_shape = jax.ShapeDtypeStruct(shape, F32)
@@ -585,9 +629,11 @@
     return pl.pallas_call(
         functools.partial(apply_kernel, wide, slices, steps),
         out_shape=(cube_shape,) * 4 + (jax.ShapeDtypeStruct((4, span, lanes), F32),),
-        in_specs=[vmem] * 10,
+        in_specs=[vmem] * 11,
         out_specs=(hbm,) * 5,
-        scratch_shapes=[cube, cube, cube, dma((steps, 3)), dma((2,))],
+        scratch_shapes=[
+            cube, cube, cube, pltpu.VMEM((4, span, lanes), F32), dma((steps, 3)), dma((2,)),
+        ],
         compiler_params=pltpu.CompilerParams(vmem_limit_bytes=16 << 20),
         name="apply",
     )(*passed)

time: 20.9 us -> 20.8 us (level)
  no operation moved by 1% of the time
where the time goes in v3:
time: 20.8 us; the launch traced here: 20.6 us
  Pallas kernels  20 us (96%)
  between operations  0.64 us (3%)
    pallas_call x1, Pallas kernels, exchange(): pl.pallas_call(functools.partial(exchange_kernel, n, n_prod, m, slices, l...  16.5 us
    pallas_call x1, Pallas kernels, apply(): pl.pallas_call(functools.partial(apply_kernel, wide, slices, steps), out_...  3.42 us

profile of v3, /device:TPU:0, one launch (start us, length us, event | category | flops | bytes accessed | tf_op | source)
XLA Modules:
  0.0 20.6 jit_solution(505560030842227854)
XLA Ops:
  0.6 16.5 %exchange.1 = (f32[128,32,128]{2,1,0:T(8,128)S(1)}, f32[128,32,128]{2,1,0:T(8,128)S(1)}, f32[128,32,128]{2,1,0:T(8,128)S(1)}, f32[128,32,128]{2,1,0:T(8,128)S(1)...) custom-call(s32[32]{0:T(128)} %week_hbm.1, ...), custom_call_target="tpu_custom_call" | custom-call | tf_op jit(solution)/shard_map/exchange/pallas_call | solution.py:517
  17.2 3.4 %apply.1 = (f32[128,32,128]{2,1,0:T(8,128)}, f32[128,32,128]{2,1,0:T(8,128)}, f32[128,32,128]{2,1,0:T(8,128)}, f32[128,32,128]{2,1,0:T(8,128)}, f32[4,32,128]{2,1,0:T(8,128)}) custom-call(f32[128,32,128]{2,1,0:T(8,128)S(1)} %get-tuple-element.16.run_in, f32[128,32,128]{2,1,0:T(8,128)S(1)} %get-tuple-element.17.week_in, ...), custom_call_target="tpu_custom_call" | custom-call | tf_op jit(solution)/shard_map/apply/pallas_call | solution.py:629

commit v4 on v3

--- a/solution.py
+++ b/solution.py
@@ -178,6 +178,7 @@
     sent += to_mates(lambda peer: send1.at[lax.rem(peer, slices)], recv1, s1_s, s1_r)
 
     linked = (me < n - 1, me > 0)
+    middle = (me == m - 1, me == m)
     aside = (lax.rem(me + 1, n), lax.rem(me + n - 1, n))
 
     def edge_copy(side, level):
@@ -196,7 +197,7 @@
 
     for side in range(2):
 
-        @pl.when(linked[side])
+        @pl.when(middle[side])
         def _():
             tile_copy(side).start()
 
@@ -375,9 +376,17 @@
 
     for side in range(2):
 
-        @pl.when(linked[1 - side])
+        @pl.when(middle[1 - side])
         def _():
             tile_copy(side).wait_recv()
+
+    @pl.when(here > 0)
+    def _():
+        beside[0] = info[lax.rem(here + m - 1, m)]
+
+    @pl.when(here < m - 1)
+    def _():
+        beside[1] = info[lax.rem(here + 1, m)]
 
     def gain(side, lane_seen, own):
         value = jnp.broadcast_to(beside[side, 7:8, lane_seen : lane_seen + 1], (1, lanes))
@@ -468,7 +477,10 @@
 
         @pl.when(linked[side])
         def _():
-            tile_copy(side).wait_send()
+            @pl.when(middle[side])
+            def _():
+                tile_copy(side).wait_send()
+
             for level in range(2):
                 edge_copy(side, level).wait_send()
 

time: 20.8 us -> 20.7 us (level)
  no operation moved by 1% of the time
where the time goes in v4:
time: 20.7 us; the launch traced here: 20.6 us
  Pallas kernels  19.9 us (96%)
  between operations  0.64 us (3%)
    pallas_call x1, Pallas kernels, exchange(): pl.pallas_call(functools.partial(exchange_kernel, n, n_prod, m, slices, l...  16.5 us
    pallas_call x1, Pallas kernels, apply(): pl.pallas_call(functools.partial(apply_kernel, wide, slices, steps), out_...  3.42 us

profile of v4, /device:TPU:0, one launch (start us, length us, event | category | flops | bytes accessed | tf_op | source)
XLA Modules:
  0.0 20.6 jit_solution(11738026890268608585)
XLA Ops:
  0.6 16.5 %exchange.1 = (f32[128,32,128]{2,1,0:T(8,128)S(1)}, f32[128,32,128]{2,1,0:T(8,128)S(1)}, f32[128,32,128]{2,1,0:T(8,128)S(1)}, f32[128,32,128]{2,1,0:T(8,128)S(1)...) custom-call(s32[32]{0:T(128)} %week_hbm.1, ...), custom_call_target="tpu_custom_call" | custom-call | tf_op jit(solution)/shard_map/exchange/pallas_call | solution.py:529
  17.2 3.4 %apply.1 = (f32[128,32,128]{2,1,0:T(8,128)}, f32[128,32,128]{2,1,0:T(8,128)}, f32[128,32,128]{2,1,0:T(8,128)}, f32[128,32,128]{2,1,0:T(8,128)}, f32[4,32,128]{2,1,0:T(8,128)}) custom-call(f32[128,32,128]{2,1,0:T(8,128)S(1)} %get-tuple-element.16.run_in, f32[128,32,128]{2,1,0:T(8,128)S(1)} %get-tuple-element.17.week_in, ...), custom_call_target="tpu_custom_call" | custom-call | tf_op jit(solution)/shard_map/apply/pallas_call | solution.py:641
